TPU v7x, 128 devices: a whole 4x4x4 slice. The times are simulated.
128 devices in a mesh: batch: 8 (over z, core), seq: 16 (over x, y).
Axes of the slice: x: 4, y: 4, z: 4, core: 2. Of those that a mesh axis runs over, the one named last changes fastest.
Arguments:
- queries: bfloat16 [65536, 8, 256], P(('batch', 'seq')), parts along dimension 0, may hold values from -400 to 400
- key_heads: bfloat16 [65536, 4, 256], P(('batch', 'seq')), parts along dimension 0, may hold values from -16 to 16
- projected_value_heads: bfloat16 [65536, 4, 256], P(('batch', 'seq')), parts along dimension 0, may hold values from -6 to 6
- lengths: int32 [8], P('batch'), parts along dimension 0, may hold values from 7681 to 8192
Outputs:
- attended: bfloat16 [65536, 8, 256], P(('batch', 'seq')), parts along dimension 0
There are 8 independent parts, one for each index of `batch`. A program takes and returns all parts, laid end to end along the dimension named above; each array names one. Nothing has to cross between parts.
All inputs are finite; a program needn't handle non-finite values.
Results may differ from a plain program's by a relative error of at most 0.0033.
Values may be sent and summed in bfloat16 or wider, within the bound.
A program may use at most 192 MiB of HBM per device.

v0:
```python
import math

import jax
import jax.numpy as jnp
from jax import lax
from jax.sharding import PartitionSpec as P

WINDOW = 4096
SINKS = 4


def broadcast(x, axis, root):
    return lax.dynamic_index_in_dim(lax.all_gather(x, axis), root, 0, keepdims=False)


def shards(queries, key_heads, projected_value_heads, lengths):
    tok_rows = queries.shape[0]
    head_count = queries.shape[1]
    head_width = queries.shape[2]
    kv_heads = key_heads.shape[1]
    share = head_count // kv_heads
    position = lax.axis_index("seq")
    length_now = lengths[0]
    first_row = position * tok_rows
    score_scale = head_width ** (-0.5)
    grouped = queries.reshape(tok_rows, kv_heads, share, head_width)
    query_pos = first_row + jnp.arange(tok_rows, dtype=jnp.int32)
    last_query = first_row + tok_rows - 1

    def attend(running, kv_block, key_start, sink_mode):
        key_count = kv_block.shape[1]
        key_pos = key_start + jnp.arange(key_count, dtype=jnp.int32)
        if sink_mode:
            useful = first_row < length_now
        else:
            useful = (
                (key_start <= last_query)
                & (key_start + key_count - 1 > first_row - WINDOW)
                & (key_start < length_now)
                & (first_row < length_now)
                & (key_start + key_count > SINKS)
            )

        def compute(current):
            maximum, totals, weighted = current
            scores = (
                jnp.einsum(
                    "qhgd,khd->hgqk", grouped, kv_block[0], preferred_element_type=jnp.float32
                )
                * score_scale
            )
            distance = query_pos[:, None] - key_pos[None, :]
            if sink_mode:
                visible = (distance >= 0) & (key_pos[None, :] < length_now)
            else:
                visible = (
                    (distance >= 0)
                    & (distance < WINDOW)
                    & (key_pos[None, :] >= SINKS)
                    & (key_pos[None, :] < length_now)
                )
            visible = visible & (query_pos[:, None] < length_now)
            masked = jnp.where(visible, scores, -1e30)
            newest = jnp.maximum(maximum, jnp.max(masked, axis=-1))
            weights = jnp.where(visible, jnp.exp(scores - newest[..., None]), 0.0)
            rescale = jnp.exp(maximum - newest)
            totals = totals * rescale + jnp.sum(weights, axis=-1)
            weighted = weighted * rescale[..., None] + jnp.einsum(
                "hgqk,khd->hgqd",
                weights.astype(jnp.bfloat16),
                kv_block[1],
                preferred_element_type=jnp.float32,
            )
            return (newest, totals, weighted)

        return lax.cond(useful, compute, lambda current: current, running)

    running = (
        jnp.full((kv_heads, share, tok_rows), -1e30, jnp.float32),
        jnp.zeros((kv_heads, share, tok_rows), jnp.float32),
        jnp.zeros((kv_heads, share, tok_rows, head_width), jnp.float32),
    )
    own_pair = jnp.stack([key_heads, projected_value_heads])
    sink_pair = broadcast(own_pair[:, :SINKS], "seq", 0)
    running = attend(running, sink_pair, jnp.int32(0), True)
    shard_piece = lax.all_gather(own_pair, "seq", axis=1, tiled=True)
    piece_rows = shard_piece.shape[1]
    block_size = math.gcd(piece_rows, tok_rows)

    def one_slice(slice_index, inner):
        sliced = lax.dynamic_slice_in_dim(shard_piece, slice_index * block_size, block_size, 1)
        return attend(inner, sliced, slice_index * block_size, False)

    running = lax.fori_loop(0, piece_rows // block_size, one_slice, running)
    maximum, totals, weighted = running
    valid = query_pos < length_now
    result = jnp.where(valid[:, None], weighted / jnp.where(valid, totals, 1.0)[..., None], 0.0)
    return (
        result.transpose(2, 0, 1, 3).reshape(tok_rows, head_count, head_width).astype(jnp.bfloat16)
    )


def solution(mesh):
    in_specs = (
        P(("batch", "seq"), None, None),
        P(("batch", "seq"), None, None),
        P(("batch", "seq"), None, None),
        P("batch"),
    )
    out_specs = P(("batch", "seq"), None, None)
    return jax.shard_map(shards, mesh=mesh, in_specs=in_specs, out_specs=out_specs, check_vma=False)
```

profile of v0, /device:TPU:70, one launch (start us, length us, event | category | flops | bytes accessed | tf_op | source)
XLA Modules:
  0.0 381.3 jit_solution(8940974404311227422)
XLA Ops:
  6.5 4.4 %pad_maximum_fusion = bf16[2,512,4,256]{3,2,1,0:T(4,128)(2,1)} fusion(bf16[1,512,4,256]{3,2,1,0:T(4,128)(2,1)} %bitcast.72, bf16[1,512,4,256]{3,2,1,0:T(4,128)(2,1)} %bitcast.70), kind=kLoop, calls=%fused_computation.57 | loop fusion | flops 1048576 | bytes 4194304 | tf_op jit(solution)/shard_map/stack | solution.py:83
  11.7 2.0 copy.11
  14.5 24.6 %all-gather = bf16[32,4,4,256]{3,2,1,0:T(4,128)(2,1)S(1)} all-gather(bf16[2,4,4,256]{3,2,1,0:T(4,128)(2,1)S(1)} %fusion.35), channel_id=2, replica_groups=mesh['batch'=8,'seq'=16] {'seq'}, dimensions={0}, use_global_device_ids=true | all-gather | bytes 278528 | tf_op jit(solution)/shard_map/all_gather | solution.py:13
  39.1 7.7 %conditional.2 = (f32[4,2,512]{2,1,0:T(2,128)}, f32[4,2,512]{2,1,0:T(2,128)S(1)}, f32[4,2,512,256]{3,2,1,0:T(8,128)}) conditional(s32[]{:T(128)} %convert_element_type.33, () %tuple.61, (s32[512]{0:T(512)S(1)}, s32[4]{0:T(128)S(1)}, s32[]{:T(128)}, s32[4]{0:T(128)S(1)}, bf16[16,2,4,4,256]{4,3,2,1,0:T(4,128)(2,1)S(1)}, ...), branch_computations={%region_0.1_spmd, %region_1.4_spmd} | conditional | flops 17998340 | bytes 7222344 | solution.py:76
  42.0 0.8 fusion.4
  42.7 0.7 fusion.12
  43.5 3.3 convolution_add_fusion
  46.8 163.7 %all-gather.3.cloned.1.call-done = bf16[2,8192,4,256]{3,2,1,0:T(4,128)(2,1)} async-done(((bf16[2,512,4,256]{3,2,1,0:T(4,128)(2,1)}), bf16[2,8192,4,256]{3,2,1,0:T(4,128)(2,1)}) %all-gather.3.cloned.1.call-update) | async-done | bytes 33554448 | tf_op jit(solution)/shard_map/all_gather | solution.py:86
  210.4 23.1 %copy.13 = bf16[2,8192,4,256]{3,1,2,0:T(8,128)(2,1)} copy(bf16[2,8192,4,256]{3,2,1,0:T(4,128)(2,1)} %all-gather.3.cloned.1.call-done) | data formatting | bytes 67108864
  233.5 135.7 %while.22 = (s32[]{:T(128)}, f32[4,2,512]{2,1,0:T(2,128)}, f32[4,2,512]{2,1,0:T(2,128)S(1)}, f32[4,2,512,256]{3,2,1,0:T(8,128)}, s32[]{:T(128)}, /*index=5*/s32[...) while((s32[]{:T(128)}, f32[4,2,512]{2,1,0:T(2,128)}, ...), condition=%wide.region_9.10_spmd.clone, body=%wide.region_4.9_spmd.clone.sunk | while | flops 2174495232 | bytes 39079348 | solution.py:94
  237.1 13.8 %conditional.5 = ((f32[4,2,512]{2,1,0:T(2,128)}, f32[4,2,512]{2,1,0:T(2,128)S(1)}, f32[4,2,512,256]{3,2,1,0:T(8,128)})) conditional(s32[]{:T(128)} %convert_element_type.46, (f32[4,2,512]{2,1,0:T(2,128)}, f32[4,2,512]{2,1,0:T(2,128)S(1)}, f32[4,2,512,256]{3,2,1,0:T(8,128)}) %tuple.89, (s32[]{:T(128)}, s32[]{:T(128)}, s32[512]{0:T(512)S(1)}, ...), branch_computations={%region_5.5_spmd, %region_6.8_spmd} | conditional | flops 2174495232 | bytes 39076968 | solution.py:76
  238.2 2.8 fusion.13
  241.7 1.7 fusion.17
  244.2 6.2 %multiply_add_fusion = f32[4,2,512,256]{3,2,1,0:T(8,128)} fusion(f32[4,2,512,256]{3,2,1,0:T(8,128)} %get-tuple-element.461, f32[4,2,512]{2,1,0:T(2,128)S(1)} %bitcast.74, f32[4,512,512,2]{2,1,3,0:T(8,128)S(1)} %get-tuple-element.568, f32[4,2,512]{2,1,0:T(2,128)S(1)} %max.4, pred[512,512]{0,1:T(8,128)(4,1)S(1)} %fusion.30, ...), kind=kOutput, calls=%fused_computation.30 | convolution fusion | flops 1084227584 | bytes 18120712 | tf_op jit(solution)/shard_map/while/body/eval_jaxpr/cond/branch_1_fun/hgqk,khd->hgqd/dot_general | solution.py:68
  251.6 13.8 %conditional.5 = ((f32[4,2,512]{2,1,0:T(2,128)}, f32[4,2,512]{2,1,0:T(2,128)S(1)}, f32[4,2,512,256]{3,2,1,0:T(8,128)})) conditional(s32[]{:T(128)} %convert_element_type.46, (f32[4,2,512]{2,1,0:T(2,128)}, f32[4,2,512]{2,1,0:T(2,128)S(1)}, f32[4,2,512,256]{3,2,1,0:T(8,128)}) %tuple.89, (s32[]{:T(128)}, s32[]{:T(128)}, s32[512]{0:T(512)S(1)}, ...), branch_computations={%region_5.5_spmd, %region_6.8_spmd} | conditional | flops 2174495232 | bytes 39076968 | solution.py:76
  252.7 2.8 fusion.13
  256.2 1.7 fusion.17
  258.7 6.2 %multiply_add_fusion = f32[4,2,512,256]{3,2,1,0:T(8,128)} fusion(f32[4,2,512,256]{3,2,1,0:T(8,128)} %get-tuple-element.461, f32[4,2,512]{2,1,0:T(2,128)S(1)} %bitcast.74, f32[4,512,512,2]{2,1,3,0:T(8,128)S(1)} %get-tuple-element.568, f32[4,2,512]{2,1,0:T(2,128)S(1)} %max.4, pred[512,512]{0,1:T(8,128)(4,1)S(1)} %fusion.30, ...), kind=kOutput, calls=%fused_computation.30 | convolution fusion | flops 1084227584 | bytes 18120712 | tf_op jit(solution)/shard_map/while/body/eval_jaxpr/cond/branch_1_fun/hgqk,khd->hgqd/dot_general | solution.py:68
  266.1 13.8 %conditional.5 = ((f32[4,2,512]{2,1,0:T(2,128)}, f32[4,2,512]{2,1,0:T(2,128)S(1)}, f32[4,2,512,256]{3,2,1,0:T(8,128)})) conditional(s32[]{:T(128)} %convert_element_type.46, (f32[4,2,512]{2,1,0:T(2,128)}, f32[4,2,512]{2,1,0:T(2,128)S(1)}, f32[4,2,512,256]{3,2,1,0:T(8,128)}) %tuple.89, (s32[]{:T(128)}, s32[]{:T(128)}, s32[512]{0:T(512)S(1)}, ...), branch_computations={%region_5.5_spmd, %region_6.8_spmd} | conditional | flops 2174495232 | bytes 39076968 | solution.py:76
  267.2 2.8 fusion.13
  270.7 1.7 fusion.17
  273.2 6.2 %multiply_add_fusion = f32[4,2,512,256]{3,2,1,0:T(8,128)} fusion(f32[4,2,512,256]{3,2,1,0:T(8,128)} %get-tuple-element.461, f32[4,2,512]{2,1,0:T(2,128)S(1)} %bitcast.74, f32[4,512,512,2]{2,1,3,0:T(8,128)S(1)} %get-tuple-element.568, f32[4,2,512]{2,1,0:T(2,128)S(1)} %max.4, pred[512,512]{0,1:T(8,128)(4,1)S(1)} %fusion.30, ...), kind=kOutput, calls=%fused_computation.30 | convolution fusion | flops 1084227584 | bytes 18120712 | tf_op jit(solution)/shard_map/while/body/eval_jaxpr/cond/branch_1_fun/hgqk,khd->hgqd/dot_general | solution.py:68
  280.6 13.8 %conditional.5 = ((f32[4,2,512]{2,1,0:T(2,128)}, f32[4,2,512]{2,1,0:T(2,128)S(1)}, f32[4,2,512,256]{3,2,1,0:T(8,128)})) conditional(s32[]{:T(128)} %convert_element_type.46, (f32[4,2,512]{2,1,0:T(2,128)}, f32[4,2,512]{2,1,0:T(2,128)S(1)}, f32[4,2,512,256]{3,2,1,0:T(8,128)}) %tuple.89, (s32[]{:T(128)}, s32[]{:T(128)}, s32[512]{0:T(512)S(1)}, ...), branch_computations={%region_5.5_spmd, %region_6.8_spmd} | conditional | flops 2174495232 | bytes 39076968 | solution.py:76
  281.8 2.8 fusion.13
  285.3 1.7 fusion.17
  287.7 6.2 %multiply_add_fusion = f32[4,2,512,256]{3,2,1,0:T(8,128)} fusion(f32[4,2,512,256]{3,2,1,0:T(8,128)} %get-tuple-element.461, f32[4,2,512]{2,1,0:T(2,128)S(1)} %bitcast.74, f32[4,512,512,2]{2,1,3,0:T(8,128)S(1)} %get-tuple-element.568, f32[4,2,512]{2,1,0:T(2,128)S(1)} %max.4, pred[512,512]{0,1:T(8,128)(4,1)S(1)} %fusion.30, ...), kind=kOutput, calls=%fused_computation.30 | convolution fusion | flops 1084227584 | bytes 18120712 | tf_op jit(solution)/shard_map/while/body/eval_jaxpr/cond/branch_1_fun/hgqk,khd->hgqd/dot_general | solution.py:68
  295.2 13.8 %conditional.5 = ((f32[4,2,512]{2,1,0:T(2,128)}, f32[4,2,512]{2,1,0:T(2,128)S(1)}, f32[4,2,512,256]{3,2,1,0:T(8,128)})) conditional(s32[]{:T(128)} %convert_element_type.46, (f32[4,2,512]{2,1,0:T(2,128)}, f32[4,2,512]{2,1,0:T(2,128)S(1)}, f32[4,2,512,256]{3,2,1,0:T(8,128)}) %tuple.89, (s32[]{:T(128)}, s32[]{:T(128)}, s32[512]{0:T(512)S(1)}, ...), branch_computations={%region_5.5_spmd, %region_6.8_spmd} | conditional | flops 2174495232 | bytes 39076968 | solution.py:76
  296.3 2.8 fusion.13
  299.8 1.7 fusion.17
  302.2 6.2 %multiply_add_fusion = f32[4,2,512,256]{3,2,1,0:T(8,128)} fusion(f32[4,2,512,256]{3,2,1,0:T(8,128)} %get-tuple-element.461, f32[4,2,512]{2,1,0:T(2,128)S(1)} %bitcast.74, f32[4,512,512,2]{2,1,3,0:T(8,128)S(1)} %get-tuple-element.568, f32[4,2,512]{2,1,0:T(2,128)S(1)} %max.4, pred[512,512]{0,1:T(8,128)(4,1)S(1)} %fusion.30, ...), kind=kOutput, calls=%fused_computation.30 | convolution fusion | flops 1084227584 | bytes 18120712 | tf_op jit(solution)/shard_map/while/body/eval_jaxpr/cond/branch_1_fun/hgqk,khd->hgqd/dot_general | solution.py:68
  309.7 13.8 %conditional.5 = ((f32[4,2,512]{2,1,0:T(2,128)}, f32[4,2,512]{2,1,0:T(2,128)S(1)}, f32[4,2,512,256]{3,2,1,0:T(8,128)})) conditional(s32[]{:T(128)} %convert_element_type.46, (f32[4,2,512]{2,1,0:T(2,128)}, f32[4,2,512]{2,1,0:T(2,128)S(1)}, f32[4,2,512,256]{3,2,1,0:T(8,128)}) %tuple.89, (s32[]{:T(128)}, s32[]{:T(128)}, s32[512]{0:T(512)S(1)}, ...), branch_computations={%region_5.5_spmd, %region_6.8_spmd} | conditional | flops 2174495232 | bytes 39076968 | solution.py:76
  310.8 2.8 fusion.13
  314.3 1.7 fusion.17
  316.8 6.2 %multiply_add_fusion = f32[4,2,512,256]{3,2,1,0:T(8,128)} fusion(f32[4,2,512,256]{3,2,1,0:T(8,128)} %get-tuple-element.461, f32[4,2,512]{2,1,0:T(2,128)S(1)} %bitcast.74, f32[4,512,512,2]{2,1,3,0:T(8,128)S(1)} %get-tuple-element.568, f32[4,2,512]{2,1,0:T(2,128)S(1)} %max.4, pred[512,512]{0,1:T(8,128)(4,1)S(1)} %fusion.30, ...), kind=kOutput, calls=%fused_computation.30 | convolution fusion | flops 1084227584 | bytes 18120712 | tf_op jit(solution)/shard_map/while/body/eval_jaxpr/cond/branch_1_fun/hgqk,khd->hgqd/dot_general | solution.py:68
  324.2 13.8 %conditional.5 = ((f32[4,2,512]{2,1,0:T(2,128)}, f32[4,2,512]{2,1,0:T(2,128)S(1)}, f32[4,2,512,256]{3,2,1,0:T(8,128)})) conditional(s32[]{:T(128)} %convert_element_type.46, (f32[4,2,512]{2,1,0:T(2,128)}, f32[4,2,512]{2,1,0:T(2,128)S(1)}, f32[4,2,512,256]{3,2,1,0:T(8,128)}) %tuple.89, (s32[]{:T(128)}, s32[]{:T(128)}, s32[512]{0:T(512)S(1)}, ...), branch_computations={%region_5.5_spmd, %region_6.8_spmd} | conditional | flops 2174495232 | bytes 39076968 | solution.py:76
  325.3 2.8 fusion.13
  328.8 1.7 fusion.17
  331.3 6.2 %multiply_add_fusion = f32[4,2,512,256]{3,2,1,0:T(8,128)} fusion(f32[4,2,512,256]{3,2,1,0:T(8,128)} %get-tuple-element.461, f32[4,2,512]{2,1,0:T(2,128)S(1)} %bitcast.74, f32[4,512,512,2]{2,1,3,0:T(8,128)S(1)} %get-tuple-element.568, f32[4,2,512]{2,1,0:T(2,128)S(1)} %max.4, pred[512,512]{0,1:T(8,128)(4,1)S(1)} %fusion.30, ...), kind=kOutput, calls=%fused_computation.30 | convolution fusion | flops 1084227584 | bytes 18120712 | tf_op jit(solution)/shard_map/while/body/eval_jaxpr/cond/branch_1_fun/hgqk,khd->hgqd/dot_general | solution.py:68
  338.7 13.8 %conditional.5 = ((f32[4,2,512]{2,1,0:T(2,128)}, f32[4,2,512]{2,1,0:T(2,128)S(1)}, f32[4,2,512,256]{3,2,1,0:T(8,128)})) conditional(s32[]{:T(128)} %convert_element_type.46, (f32[4,2,512]{2,1,0:T(2,128)}, f32[4,2,512]{2,1,0:T(2,128)S(1)}, f32[4,2,512,256]{3,2,1,0:T(8,128)}) %tuple.89, (s32[]{:T(128)}, s32[]{:T(128)}, s32[512]{0:T(512)S(1)}, ...), branch_computations={%region_5.5_spmd, %region_6.8_spmd} | conditional | flops 2174495232 | bytes 39076968 | solution.py:76
  339.8 2.8 fusion.13
  343.3 1.7 fusion.17
  345.8 6.2 %multiply_add_fusion = f32[4,2,512,256]{3,2,1,0:T(8,128)} fusion(f32[4,2,512,256]{3,2,1,0:T(8,128)} %get-tuple-element.461, f32[4,2,512]{2,1,0:T(2,128)S(1)} %bitcast.74, f32[4,512,512,2]{2,1,3,0:T(8,128)S(1)} %get-tuple-element.568, f32[4,2,512]{2,1,0:T(2,128)S(1)} %max.4, pred[512,512]{0,1:T(8,128)(4,1)S(1)} %fusion.30, ...), kind=kOutput, calls=%fused_computation.30 | convolution fusion | flops 1084227584 | bytes 18120712 | tf_op jit(solution)/shard_map/while/body/eval_jaxpr/cond/branch_1_fun/hgqk,khd->hgqd/dot_general | solution.py:68
  353.2 13.8 %conditional.5 = ((f32[4,2,512]{2,1,0:T(2,128)}, f32[4,2,512]{2,1,0:T(2,128)S(1)}, f32[4,2,512,256]{3,2,1,0:T(8,128)})) conditional(s32[]{:T(128)} %convert_element_type.46, (f32[4,2,512]{2,1,0:T(2,128)}, f32[4,2,512]{2,1,0:T(2,128)S(1)}, f32[4,2,512,256]{3,2,1,0:T(8,128)}) %tuple.89, (s32[]{:T(128)}, s32[]{:T(128)}, s32[512]{0:T(512)S(1)}, ...), branch_computations={%region_5.5_spmd, %region_6.8_spmd} | conditional | flops 2174495232 | bytes 39076968 | solution.py:76
  354.4 2.8 fusion.13
  357.9 1.7 fusion.17
  360.3 6.2 %multiply_add_fusion = f32[4,2,512,256]{3,2,1,0:T(8,128)} fusion(f32[4,2,512,256]{3,2,1,0:T(8,128)} %get-tuple-element.461, f32[4,2,512]{2,1,0:T(2,128)S(1)} %bitcast.74, f32[4,512,512,2]{2,1,3,0:T(8,128)S(1)} %get-tuple-element.568, f32[4,2,512]{2,1,0:T(2,128)S(1)} %max.4, pred[512,512]{0,1:T(8,128)(4,1)S(1)} %fusion.30, ...), kind=kOutput, calls=%fused_computation.30 | convolution fusion | flops 1084227584 | bytes 18120712 | tf_op jit(solution)/shard_map/while/body/eval_jaxpr/cond/branch_1_fun/hgqk,khd->hgqd/dot_general | solution.py:68
  369.2 2.6 select_convert_fusion
  371.9 2.5 copy.20
  (92 shorter events, 32.0 us)
Async XLA Ops:
  6.5 203.9 %all-gather.3.cloned.1.call-start = ((), (), s32[]{:S(2)}) async-start(), calls=%async_computation | async-start | bytes 35651584 | tf_op jit(solution)/shard_map/all_gather | solution.py:86
  11.0 2.8 copy-start
Sparse Core Ops, SparseCore 0:
  11.1 199.2 all-gather.2
where the time goes:
time: 384 us; the launch traced here: 381 us
  waiting for transfers between devices  164 us (43%)
  matrix products  84.2 us (22%)
  other arithmetic  49.8 us (13%)
  local copies, waits for them, and re-layouts  33.1 us (9%)
  blocking collectives  24.6 us (6%)
  between operations  14.2 us (4%)
  loops' own time  11.7 us (3%)
    all_gather x1, waiting for transfers between devices, shards(): shard_piece = lax.all_gather(own_pair, 'seq', axis=1, tiled=True)  164 us
    dot_general x10, matrix products, compute(): jnp.einsum('hgqk,khd->hgqd', weights.astype(jnp.bfloat16), kv_block[1], p...  58.7 us
    dot_general x10, matrix products, compute(): jnp.einsum('qhgd,khd->hgqk', grouped, kv_block[0], preferred_element_type...  25.5 us
    unnamed x4, local copies, waits for them, and re-layouts  25.1 us
    all_gather x1, blocking collectives, broadcast(): lax.all_gather(x, axis)  24.6 us
    reduce_sum x10, other arithmetic, compute(): totals = totals * rescale + jnp.sum(weights, axis=-1)  16.4 us
    another operation x1, loops' own time, shards(): running = lax.fori_loop(0, piece_rows // block_size, one_slice, running)  10.9 us
  transfers between devices with their start and end apart: 1, of which 1 were waited for; matrix products, arithmetic and copies ran while one was open for 3% of the time, Pallas kernels for 0%

commit v1 on v0

v1 whole, which is shorter than its diff:
```python
import functools

import jax
import jax.numpy as jnp
from jax import lax
from jax.experimental import pallas as pl
from jax.experimental.pallas import tpu as pltpu
from jax.sharding import PartitionSpec as P

WINDOW = 4096
SINKS = 4
SIDE = 4
BLOCK = 512
HALF = 256
DIM = 256
NM = 4
NP = 8 - NM
C = 1.4426950408889634 / 16.0
NEG = -1e30
KV, Q, O = 0, 1, 2


def kernel(
    len_ref, q_in, kv_in, o_ref,
    kvb, qb, ob, relay, rx, snk, acc, mx, ls,
    ys, yr, xs, xr, ps, pr, ms, mr, ns, nr, ss, sr, loc,
):
    sid = lax.axis_index("seq")
    x = lax.div(sid, SIDE)
    y = lax.rem(sid, SIDE)
    right = lax.rem(y + 1, SIDE)
    left = lax.rem(y + 3, SIDE)
    far = lax.rem(y + 2, SIDE)
    down = lax.rem(x + 1, SIDE)
    up = lax.rem(x + 3, SIDE)

    def dev(xx, yy):
        return {"seq": xx * SIDE + yy}

    def remote(src, dst, s, r, where):
        return pltpu.make_async_remote_copy(
            src_ref=src, dst_ref=dst, send_sem=s, recv_sem=r,
            device_id=where, device_id_type=pl.DeviceIdType.MESH,
        )

    def src(p, n, half):
        if p == KV:
            return kv_in.at[n, half]
        if p == Q:
            return q_in.at[n, half]
        return ob.at[2 * n + half]

    def dst(p, n, half):
        if p == KV:
            return kvb.at[16 + 2 * n + half]
        if p == Q:
            return qb.at[2 * n + half]
        return o_ref.at[n, half]

    def peer(side):
        return right if side == 0 else left

    def direct(p, side, half):
        n = peer(side)
        k = 2 * side + half
        return remote(src(p, n, half), dst(p, y, half), ys.at[p, k], yr.at[p, k], dev(x, n))

    def relay_out(p, side):
        k = 4 + side
        return remote(
            src(p, far, side), relay.at[p, side], ys.at[p, k], yr.at[p, k], dev(x, peer(side))
        )

    def forward(p, side):
        k = 6 + side
        return remote(
            relay.at[p, side], dst(p, peer(1 - side), side), ys.at[p, k], yr.at[p, k],
            dev(x, peer(side)),
        )

    def got_direct(p, side, half):
        k = 2 * side + half
        d = dst(p, peer(1 - side), half)
        remote(d, d, ys.at[p, k], yr.at[p, k], dev(x, peer(1 - side))).wait_recv()

    def got_relay(p, side):
        k = 4 + side
        d = relay.at[p, side]
        remote(d, d, ys.at[p, k], yr.at[p, k], dev(x, peer(1 - side))).wait_recv()

    def got_forward(p, side):
        k = 6 + side
        d = dst(p, far, side)
        remote(d, d, ys.at[p, k], yr.at[p, k], dev(x, peer(1 - side))).wait_recv()

    def x_next(i):
        return remote(kvb.at[16 + i], kvb.at[8 + i], xs.at[i], xr.at[i], dev(down, y))

    def x_plus(i):
        return remote(kvb.at[8 + i], kvb.at[i], ps.at[i], pr.at[i], dev(down, y))

    def x_minus(i):
        return remote(kvb.at[16 + i], rx.at[i - NP], ms.at[i - NP], mr.at[i - NP], dev(up, y))

    def x_wrap(j):
        return remote(rx.at[j], kvb.at[NP + j], ns.at[j], nr.at[j], dev(up, y))

    def x_sink(first):
        return remote(
            kvb.at[16, :, pl.ds(0, 16), :] if first else snk, snk, ss.at[0], sr.at[0], dev(up, y)
        )

    def x_send(i):
        @pl.when(x < 3)
        def _():
            x_next(i).start()

        @pl.when((x < 2) & (i >= NP))
        def _():
            x_minus(i).start()

    relays_plus = (x == 1) | (x == 2)
    relays_wrap = (x == 0) | (x == 3)
    two_back = x >= 2

    lane = lax.broadcasted_iota(jnp.int32, (BLOCK, 128), 1)
    row = lax.rem(lax.broadcasted_iota(jnp.int32, (BLOCK, 128), 0), HALF)

    def update(yq, half, s_parts, v):
        top = s_parts[0]
        for part in s_parts[1:]:
            top = jnp.maximum(top, part)
        old = mx[yq, half]
        new = jnp.maximum(old, jnp.max(top, axis=-1, keepdims=True))
        alpha = jnp.exp2((old - new) * C)
        p_parts = [jnp.exp2((part - new) * C) for part in s_parts]
        total = p_parts[0]
        for part in p_parts[1:]:
            total = total + part
        ls[yq, half] = ls[yq, half] * alpha + total
        mx[yq, half] = new
        weights = jnp.concatenate([part.astype(jnp.bfloat16) for part in p_parts], axis=1)
        scale = jnp.concatenate([alpha, alpha], axis=1)
        acc[yq, half] = acc[yq, half] * scale + jnp.dot(
            weights, v, preferred_element_type=jnp.float32
        )

    def scores(yq, half, k):
        q = qb[2 * yq + half].reshape(BLOCK, DIM)
        return lax.dot_general(
            q, k, (((1,), (1,)), ((), ())), preferred_element_type=jnp.float32
        )

    def task(yq, b, masked):
        k = kvb[pl.ds(2 * b, 2), 0].reshape(BLOCK, DIM)
        v = kvb[pl.ds(2 * b, 2), 1].reshape(BLOCK, DIM)
        for half in range(2):
            s = scores(yq, half, k)
            parts = [s[:, 128 * j : 128 * (j + 1)] for j in range(4)]
            if masked:
                base = (8 + yq - b) * BLOCK + half * HALF
                first = jnp.where((x == 2) & (b == 0), SINKS, 0)
                for j in range(4):
                    key = lane + 128 * j
                    delta = base + row - key
                    ok = (delta >= 0) & (delta < WINDOW) & (key >= first)
                    parts[j] = jnp.where(ok, parts[j], NEG)
            update(yq, half, parts, v)

    def sink_task(yq):
        k = jnp.concatenate([snk[0], jnp.zeros((112, DIM), jnp.bfloat16)], axis=0)
        v = jnp.concatenate([snk[1], jnp.zeros((112, DIM), jnp.bfloat16)], axis=0)
        for half in range(2):
            s = jnp.where(lane < SINKS, scores(yq, half, k), NEG)
            update(yq, half, [s], v)

    def loop(n, body):
        def step(t, carry):
            body(t)
            return carry

        lax.fori_loop(0, n, step, 0)

    def finalize(yq):
        length = len_ref[0]
        for half in range(2):
            inv = 1.0 / jnp.sum(ls[yq, half], axis=-1, keepdims=True)
            first = (x * SIDE + yq) * BLOCK + half * HALF
            ok = first + row < length
            ok = jnp.concatenate([ok, ok], axis=1)
            out = jnp.where(ok, acc[yq, half] * inv, 0.0)
            ob[2 * yq + half] = out.astype(jnp.bfloat16).reshape(2, HALF, DIM)

    def own_out(half):
        return pltpu.make_async_copy(ob.at[2 * y + half], o_ref.at[y, half], loc.at[half])

    def send_out(yq):
        @pl.when(y == yq)
        def _():
            for half in range(2):
                own_out(half).start()

        @pl.when(right == yq)
        def _():
            for half in range(2):
                direct(O, 0, half).start()

        @pl.when(left == yq)
        def _():
            for half in range(2):
                direct(O, 1, half).start()

        @pl.when(far == yq)
        def _():
            for side in range(2):
                relay_out(O, side).start()

    barrier = pltpu.get_barrier_semaphore()
    for where in (dev(x, right), dev(x, left), dev(down, y), dev(up, y)):
        pl.semaphore_signal(barrier, inc=1, device_id=where, device_id_type=pl.DeviceIdType.MESH)
    pl.semaphore_wait(barrier, 4)

    for half in range(2):
        for side in range(2):
            direct(KV, side, half).start()
    mine = [
        pltpu.make_async_copy(kv_in.at[y, half], kvb.at[16 + 2 * y + half], loc.at[2 + half])
        for half in range(2)
    ] + [
        pltpu.make_async_copy(q_in.at[y, half], qb.at[2 * y + half], loc.at[4 + half])
        for half in range(2)
    ]
    for copy in mine:
        copy.start()
    for side in range(2):
        relay_out(KV, side).start()
    for side in range(2):
        direct(Q, side, 0).start()
    for half in range(2):
        mine[half].wait()
        x_send(2 * y + half)

    def init(t):
        for half in range(2):
            mx[t, half] = jnp.full((BLOCK, 128), NEG, jnp.float32)
            ls[t, half] = jnp.zeros((BLOCK, 128), jnp.float32)
            acc[t, half] = jnp.zeros((BLOCK, DIM), jnp.float32)

    loop(SIDE, init)
    for half in range(2):
        for side in range(2):
            got_direct(KV, side, half)
            x_send(2 * peer(1 - side) + half)
    for side in range(2):
        got_relay(KV, side)
        forward(KV, side).start()
    for side in range(2):
        direct(Q, side, 1).start()
    for side in range(2):
        relay_out(Q, side).start()
    mine[2].wait()
    mine[3].wait()
    task(y, 8 + y, True)
    for side in range(2):
        got_forward(KV, side)
        x_send(2 * far + side)

    @pl.when(x == 0)
    def _():
        x_sink(True).start()

    @pl.when(x == 3)
    def _():
        x_sink(False).wait_recv()
        x_sink(False).start()

    @pl.when(relays_wrap)
    def _():
        for j in range(NM):
            x_minus(NP + j).wait_recv()
            x_wrap(j).start()

    loop(y, lambda t: task(y, 8 + t, False))
    for side in range(2):
        for half in range(2):
            got_direct(Q, side, half)

    def neighbour_block(t):
        yq = jnp.where(t == 0, left, right)
        task(yq, 8 + yq, True)
        loop(yq, lambda r: task(yq, 8 + r, False))

    loop(2, neighbour_block)
    for side in range(2):
        got_relay(Q, side)
        forward(Q, side).start()

    near = lambda t: jnp.where(t == 0, y, jnp.where(t == 1, left, right))

    @pl.when(x >= 1)
    def _():
        for n in (y, left, right):
            for half in range(2):
                x_next(2 * n + half).wait_recv()
        loop(9, lambda t: task(near(lax.div(t, 3)), 4 + near(lax.rem(t, 3)), False))
        for half in range(2):
            x_next(2 * far + half).wait_recv()

    @pl.when(relays_plus)
    def _():
        for i in reversed(range(NP)):
            x_plus(i).start()

    for side in range(2):
        got_forward(Q, side)
    task(far, 8 + far, True)
    loop(far, lambda r: task(far, 8 + r, False))

    @pl.when(x >= 1)
    def _():
        def rest(t):
            yq = jnp.where(t < 4, far, near(t - 4))
            n = jnp.where(t < 3, near(t), far)
            task(yq, 4 + n, False)

        loop(7, rest)

    @pl.when(two_back)
    def _():
        @pl.when(x == 2)
        def _():
            x_sink(False).wait_recv()

        loop(SIDE, sink_task)
        for j in range(NM):
            x_wrap(j).wait_recv()
        loop(2, lambda t: task(3 - t, 3 - t, True))
        loop(
            5,
            lambda t: task(
                jnp.where(t < 3, 2 - t, 4 - t), jnp.where(t < 3, 3, 2), False
            ),
        )

    for yq in (3, 2):
        finalize(yq)
        send_out(yq)

    def forward_out(late):
        for side in range(2):
            n = peer(side)

            @pl.when((n < 2) if late else (n >= 2))
            def _():
                got_relay(O, side)
                forward(O, side).start()

    @pl.when(two_back)
    def _():
        x_plus(3).wait_recv()
        x_plus(2).wait_recv()
        task(jnp.int32(0), jnp.int32(1), False)
        task(jnp.int32(1), jnp.int32(1), True)

    finalize(1)
    send_out(1)
    forward_out(False)

    @pl.when(two_back)
    def _():
        x_plus(1).wait_recv()
        x_plus(0).wait_recv()
        task(jnp.int32(0), jnp.int32(0), True)

    finalize(0)
    send_out(0)
    forward_out(True)

    for side in range(2):
        for half in range(2):
            got_direct(O, side, half)
        got_forward(O, side)
    for half in range(2):
        own_out(half).wait()
    for p in (KV, Q, O):
        for side in range(2):
            for half in range(2):
                direct(p, side, half).wait_send()
            relay_out(p, side).wait_send()
            forward(p, side).wait_send()

    @pl.when(x < 3)
    def _():
        for i in range(8):
            x_next(i).wait_send()

    @pl.when(relays_plus)
    def _():
        for i in range(NP):
            x_plus(i).wait_send()

    @pl.when(x < 2)
    def _():
        for i in range(NP, 8):
            x_minus(i).wait_send()

    @pl.when(relays_wrap)
    def _():
        for j in range(NM):
            x_wrap(j).wait_send()
        x_sink(False).wait_send()


def attend(lengths, q, kv):
    bf = jnp.bfloat16
    dma = pltpu.SemaphoreType.DMA
    any_space = pl.BlockSpec(memory_space=pl.ANY)
    return pl.pallas_call(
        kernel,
        name="window_attention",
        out_shape=jax.ShapeDtypeStruct(q.shape, bf),
        in_specs=[pl.BlockSpec(memory_space=pltpu.SMEM), any_space, any_space],
        out_specs=any_space,
        scratch_shapes=[
            pltpu.VMEM((24, 2, HALF, DIM), bf),
            pltpu.VMEM((8, 2, HALF, DIM), bf),
            pltpu.VMEM((8, 2, HALF, DIM), bf),
            pltpu.VMEM((3, 2, 2, HALF, DIM), bf),
            pltpu.VMEM((NM, 2, HALF, DIM), bf),
            pltpu.VMEM((2, 16, DIM), bf),
            pltpu.VMEM((SIDE, 2, BLOCK, DIM), jnp.float32),
            pltpu.VMEM((SIDE, 2, BLOCK, 128), jnp.float32),
            pltpu.VMEM((SIDE, 2, BLOCK, 128), jnp.float32),
            dma((3, 8)), dma((3, 8)),
            dma((8,)), dma((8,)),
            dma((NP,)), dma((NP,)),
            dma((NM,)), dma((NM,)),
            dma((NM,)), dma((NM,)),
            dma((1,)), dma((1,)),
            dma((6,)),
        ],
        compiler_params=pltpu.CompilerParams(
            collective_id=0, has_side_effects=True, vmem_limit_bytes=56 * 1024 * 1024
        ),
    )(lengths, q, kv)


def shards(queries, key_heads, projected_value_heads, lengths):
    tok = queries.shape[0]
    q = queries.reshape(2, HALF, SIDE, 2, DIM).transpose(2, 0, 3, 1, 4)
    kv = jnp.stack([key_heads, projected_value_heads]).reshape(2, 2, HALF, SIDE, DIM)
    kv = kv.transpose(3, 1, 0, 2, 4)
    out = attend(lengths, q, kv)
    return out.transpose(1, 3, 0, 2, 4).reshape(tok, 2 * SIDE, DIM)


def solution(mesh):
    in_specs = (
        P(("batch", "seq"), None, None),
        P(("batch", "seq"), None, None),
        P(("batch", "seq"), None, None),
        P("batch"),
    )
    out_specs = P(("batch", "seq"), None, None)
    return jax.shard_map(shards, mesh=mesh, in_specs=in_specs, out_specs=out_specs, check_vma=False)
```

time: 384 us -> 132 us (0.34)
  waiting for transfers between devices: 164 us -> 0 us
  Pallas kernels: 0 us -> 121 us
  matrix products: 84.2 us -> 0 us
  other arithmetic: 49.8 us -> 1.53 us
  local copies, waits for them, and re-layouts: 33.1 us -> 8.45 us
  blocking collectives: 24.6 us -> 0 us
  between operations: 14.2 us -> 0.79 us
  loops' own time: 11.7 us -> 0 us
    all_gather x1 -> x0, waiting for transfers between devices: 164 us -> none  [shards(): shard_piece = lax.all_gather(own_pair, 'seq', axis=1, tiled=True)]
    pallas_call x0 -> x1, Pallas kernels: none -> 121 us  [attend(): pl.pallas_call(kernel, name='window_attention', out_shape=jax.ShapeDtypeS...]
    dot_general x20 -> x0, matrix products: 84.2 us -> none  [the longest x10 58.7 us: compute(): jnp.einsum('hgqk,khd->hgqd', weights.astype(jnp.bfloat16), kv_block[1], p...]
    all_gather x1 -> x0, blocking collectives: 24.6 us -> none  [broadcast(): lax.all_gather(x, axis)]
    unnamed x4 -> x7, local copies, waits for them, and re-layouts: 25.1 us -> 2.75 us
    reduce_sum x10 -> x0, other arithmetic: 16.4 us -> none  [compute(): totals = totals * rescale + jnp.sum(weights, axis=-1)]
    another operation x18 -> x0, loops' own time: 11.7 us -> none  [the longest x1 10.9 us: shards(): running = lax.fori_loop(0, piece_rows // block_size, one_slice, running)]
    add x11 -> x0, other arithmetic: 7.33 us -> none  [the longest x10 7.33 us: compute(): totals = totals * rescale + jnp.sum(weights, axis=-1)]
  transfers between devices with their start and end apart: 1 -> 0, of which waited for: 1 -> 0; matrix products, arithmetic and copies ran while one was open for 3% -> 0% of each run, Pallas kernels for 0% -> 0%
where the time goes in v1:
time: 132 us; the launch traced here: 131 us
  Pallas kernels  121 us (92%)
  local copies, waits for them, and re-layouts  8.45 us (6%)
  other arithmetic  1.53 us (1%)
    pallas_call x1, Pallas kernels, attend(): pl.pallas_call(kernel, name='window_attention', out_shape=jax.ShapeDtypeS...  121 us
    unnamed x7, local copies, waits for them, and re-layouts  2.75 us

profile of v1, /device:TPU:70, one launch (start us, length us, event | category | flops | bytes accessed | tf_op | source)
XLA Modules:
  0.0 131.5 jit_solution(11710187318730604544)
XLA Ops:
  0.0 0.0 copy-start.1
  0.7 1.4 %copy.9 = bf16[512,4,256]{2,0,1:T(8,128)(2,1)S(1)} copy(bf16[512,4,256]{2,1,0:T(4,128)(2,1)} %param.5) | data formatting | bytes 2097152 | tf_op args[1]
  2.1 0.0 copy-done.1
  2.1 0.1 copy.10
  2.3 0.0 copy-start
  2.3 1.5 %maximum_bitcast_fusion.kv_in = bf16[4,2,2,256,256]{4,3,2,1,0:T(8,128)(2,1)} fusion(bf16[1,2,256,4,256]{4,2,0,1,3:T(8,128)(2,1)S(1)} %bitcast.15, bf16[1,2,256,4,256]{4,2,0,1,3:T(8,128)(2,1)S(1)} %bitcast.14), kind=kLoop, calls=%fused_computation | loop fusion | flops 1048576 | bytes 4194304 | tf_op jit(solution)/shard_map/transpose | solution.py:452
  3.8 0.8 copy-done
  4.6 0.4 copy.7
  5.0 1.5 %copy.14 = bf16[2,256,4,2,256]{4,1,3,0,2:T(8,128)(2,1)} copy(bf16[2,256,4,2,256]{4,1,0,3,2:T(8,128)(2,1)S(1)} %bitcast.13) | data formatting | bytes 4194304 | tf_op jit(solution)/shard_map/reshape | solution.py:450
  6.5 120.7 %window_attention.1 = bf16[4,2,2,256,256]{4,3,2,1,0:T(8,128)(2,1)} custom-call(s32[1]{0:T(128)S(6)} %copy.15.len_ref, bf16[4,2,2,256,256]{4,3,2,1,0:T(8,128)(2,1)} %bitcast.10, bf16[4,2,2,256,256]{4,3,2,1,0:T(8,128)(2,1)} %maximum_bitcast_fusion.kv_in), custom_call_target="tpu_custom_call" | custom-call | tf_op jit(solution)/shard_map/window_attention/pallas_call | solution.py:418
  127.2 1.7 %copy.11 = bf16[2,256,4,2,256]{4,1,0,3,2:T(8,128)(2,1)S(1)} copy(bf16[2,256,4,2,256]{4,1,3,0,2:T(8,128)(2,1)} %bitcast.11) | data formatting | bytes 4194304 | tf_op jit(solution)/shard_map/transpose | solution.py:454
  129.0 2.5 %copy.12 = bf16[512,8,256]{2,1,0:T(8,128)(2,1)} copy(bf16[512,8,256]{2,0,1:T(8,128)(2,1)S(1)} %bitcast.12) | data formatting | bytes 4194304 | tf_op jit(solution)/shard_map/reshape | solution.py:454
Async XLA Ops:
  0.0 2.1 %copy-start.1 = (bf16[512,4,256]{2,1,0:T(4,128)(2,1)S(1)}, bf16[512,4,256]{2,1,0:T(4,128)(2,1)}, u32[]{:S(2)}) copy-start(bf16[512,4,256]{2,1,0:T(4,128)(2,1)} %param.6) | copy-start | bytes 3145732
  2.3 2.4 %copy-start = (bf16[512,8,256]{2,1,0:T(8,128)(2,1)S(1)}, bf16[512,8,256]{2,1,0:T(8,128)(2,1)}, u32[]{:S(2)}) copy-start(bf16[512,8,256]{2,1,0:T(8,128)(2,1)} %param.4) | copy-start | bytes 6291460

commit v2 on v1

v2 whole, which is shorter than its diff:
```python
import functools

import jax
import jax.numpy as jnp
from jax import lax
from jax.experimental import pallas as pl
from jax.experimental.pallas import tpu as pltpu
from jax.sharding import PartitionSpec as P

SINKS = 4
SIDE = 4
BLOCK = 512
HALF = 256
DIM = 256
NM = 5
NP = 8 - NM
C = 1.4426950408889634 / 16.0
NEG = -1e30
K, V, Q, O = 0, 1, 2, 3
FULL, DIAG, EDGE = 0, 1, 2


def kernel(
    len_ref, q_in, k_in, v_in, o_ref,
    kvb, qb, ob, rx, snk, acc0, acc1, mx0, mx1, ls0, ls1, sc0, sc1,
    ys, yr, xs, xr, ps, pr, ms, mr, ns, nr, ss, sr, loc,
):
    accs, mxs, lss, scs = (acc0, acc1), (mx0, mx1), (ls0, ls1), (sc0, sc1)
    sid = lax.axis_index("seq")
    x = lax.div(sid, SIDE)
    y = lax.rem(sid, SIDE)
    right = lax.rem(y + 1, SIDE)
    left = lax.rem(y + 3, SIDE)
    far = lax.rem(y + 2, SIDE)
    down = lax.rem(x + 1, SIDE)
    up = lax.rem(x + 3, SIDE)

    def dev(xx, yy):
        return {"seq": xx * SIDE + yy}

    def remote(src, dst, s, r, where):
        return pltpu.make_async_remote_copy(
            src_ref=src, dst_ref=dst, send_sem=s, recv_sem=r,
            device_id=where, device_id_type=pl.DeviceIdType.MESH,
        )

    def rows(half):
        return pl.ds(half * HALF, HALF)

    def src(p, n, half):
        if p == K:
            return k_in.at[n, rows(half)]
        if p == V:
            return v_in.at[n, rows(half)]
        if p == Q:
            return q_in.at[pl.ds(2 * n, 2), rows(half)]
        return ob.at[2 * n + half]

    def dst(p, n, half):
        if p in (K, V):
            return kvb.at[16 + 2 * n + half, p]
        if p == Q:
            return qb.at[2 * n + half]
        return o_ref.at[pl.ds(2 * n, 2), rows(half)]

    to = (right, left, far)
    come = (left, right, far)

    def send(p, side, half):
        k = 2 * side + half
        return remote(
            src(p, to[side], half), dst(p, y, half), ys.at[p, k], yr.at[p, k], dev(x, to[side])
        )

    def got(p, side, half):
        k = 2 * side + half
        d = dst(p, come[side], half)
        remote(d, d, ys.at[p, k], yr.at[p, k], dev(x, come[side])).wait_recv()

    def x_next(i):
        return remote(kvb.at[16 + i], kvb.at[8 + i], xs.at[i], xr.at[i], dev(down, y))

    def x_plus(i):
        return remote(kvb.at[8 + i], kvb.at[i], ps.at[i], pr.at[i], dev(down, y))

    def x_minus(i):
        return remote(kvb.at[16 + i], rx.at[i - NP], ms.at[i - NP], mr.at[i - NP], dev(up, y))

    def x_wrap(j):
        return remote(rx.at[j], kvb.at[NP + j], ns.at[j], nr.at[j], dev(up, y))

    def x_sink(first):
        return remote(
            kvb.at[16, :, pl.ds(0, 16), :] if first else snk, snk, ss.at[0], sr.at[0], dev(up, y)
        )

    def x_send(i):
        @pl.when(x < 3)
        def _():
            x_next(i).start()

        @pl.when((x < 2) & (i >= NP))
        def _():
            x_minus(i).start()

    relays_plus = (x == 1) | (x == 2)
    relays_wrap = (x == 0) | (x == 3)
    two_back = x >= 2

    lane = lax.broadcasted_iota(jnp.int32, (BLOCK, 128), 1)
    row = lax.rem(lax.broadcasted_iota(jnp.int32, (BLOCK, 128), 0), HALF)

    def scores(yq, half, k):
        q = qb[2 * yq + half].reshape(BLOCK, DIM)
        return lax.dot_general(
            q, k, (((1,), (1,)), ((), ())), preferred_element_type=jnp.float32
        )

    def update(yq, half, parts, v):
        acc, mx, ls = accs[half], mxs[half], lss[half]
        top = parts[0]
        for part in parts[1:]:
            top = jnp.maximum(top, part)
        old = mx[yq]
        new = jnp.maximum(old, jnp.max(top, axis=-1, keepdims=True))
        alpha = jnp.exp2((old - new) * C)
        weights = [jnp.exp2((part - new) * C) for part in parts]
        total = weights[0]
        for part in weights[1:]:
            total = total + part
        ls[yq] = ls[yq] * alpha + total
        mx[yq] = new
        rounded = jnp.concatenate([part.astype(jnp.bfloat16) for part in weights], axis=1)
        scale = jnp.concatenate([alpha, alpha], axis=1)
        acc[yq] = acc[yq] * scale + jnp.dot(rounded, v, preferred_element_type=jnp.float32)

    def cols(s):
        return [s[:, 128 * j : 128 * (j + 1)] for j in range(s.shape[1] // 128)]

    def keys_of(piece, n):
        return kvb[pl.ds(piece, n), 0].reshape(n * HALF, DIM)

    def values_of(piece, n):
        return kvb[pl.ds(piece, n), 1].reshape(n * HALF, DIM)

    def tiles(yq, half, piece, modes):
        n = len(modes)
        parts = cols(scores(yq, half, keys_of(piece, n)))
        for j in range(2 * n):
            key = lane + 128 * (j % 2)
            if modes[j // 2] == DIAG:
                parts[j] = jnp.where(key <= row, parts[j], NEG)
            if modes[j // 2] == EDGE:
                ok = key > row
                if half == 0 and j == 0:
                    ok = ok & (key >= jnp.where((x == 2) & (yq == 0), SINKS, 0))
                parts[j] = jnp.where(ok, parts[j], NEG)
        update(yq, half, parts, values_of(piece, n))

    def diag(yq):
        tiles(yq, 0, 16 + 2 * yq, [DIAG])
        tiles(yq, 1, 16 + 2 * yq, [FULL, DIAG])

    def edge(yq):
        tiles(yq, 0, 2 * yq, [EDGE, FULL])
        tiles(yq, 1, 2 * yq + 1, [EDGE])

    def loop(n, body):
        def step(t, carry):
            body(t)
            return carry

        lax.fori_loop(0, n, step, 0)

    def pipe(n, get):
        def qk(t, half):
            yq, b = get(t)
            scs[half][...] = scores(yq, half, keys_of(2 * b, 2))

        def softmax(t, half):
            yq, b = get(t)
            update(yq, half, cols(scs[half][...]), values_of(2 * b, 2))

        def step(t):
            qk(t, 1)
            softmax(t, 0)
            qk(jnp.minimum(t + 1, n - 1), 0)
            softmax(t, 1)

        @pl.when(n > 0)
        def _():
            qk(0, 0)
            loop(n, step)

    def sink_task(yq):
        pad = jnp.zeros((112, DIM), jnp.bfloat16)
        k = jnp.concatenate([snk[0], pad], axis=0)
        v = jnp.concatenate([snk[1], pad], axis=0)
        for half in range(2):
            update(yq, half, [jnp.where(lane < SINKS, scores(yq, half, k), NEG)], v)

    def finalize(yq, half):
        inv = 1.0 / jnp.sum(lss[half][yq], axis=-1, keepdims=True)
        ok = (x * SIDE + yq) * BLOCK + half * HALF + row < len_ref[0]
        ok = jnp.concatenate([ok, ok], axis=1)
        out = jnp.where(ok, accs[half][yq] * inv, 0.0)
        ob[2 * yq + half] = out.astype(jnp.bfloat16).reshape(2, HALF, DIM)

    def own_out(half):
        return pltpu.make_async_copy(ob.at[2 * y + half], dst(O, y, half), loc.at[half])

    def send_out(yq, half):
        @pl.when(y == yq)
        def _():
            own_out(half).start()

        for side in range(3):

            @pl.when(to[side] == yq)
            def _():
                send(O, side, half).start()

    barrier = pltpu.get_barrier_semaphore()
    for where in (dev(x, right), dev(x, left), dev(x, far), dev(down, y), dev(up, y)):
        pl.semaphore_signal(barrier, inc=1, device_id=where, device_id_type=pl.DeviceIdType.MESH)
    pl.semaphore_wait(barrier, 5)

    mine = [
        pltpu.make_async_copy(src(p, y, half), dst(p, y, half), loc.at[2 + 2 * p + half])
        for p in (K, V, Q)
        for half in range(2)
    ]
    for half in range(2):
        for side in range(2):
            send(K, side, half).start()
            send(V, side, half).start()
    for copy in mine:
        copy.start()
    for half in range(2):
        for side in range(2):
            send(Q, side, half).start()
    for half in range(2):
        send(K, 2, half).start()
        send(V, 2, half).start()
    for half in range(2):
        send(Q, 2, half).start()
    for half in range(2):
        mine[half].wait()
        mine[2 + half].wait()
        x_send(2 * y + half)

    def init(t):
        for half in range(2):
            mxs[half][t] = jnp.full((BLOCK, 128), NEG, jnp.float32)
            lss[half][t] = jnp.zeros((BLOCK, 128), jnp.float32)
            accs[half][t] = jnp.zeros((BLOCK, DIM), jnp.float32)

    loop(SIDE, init)
    mine[4].wait()
    mine[5].wait()
    diag(y)
    for side in range(2):
        for half in range(2):
            got(K, side, half)
            got(V, side, half)
            x_send(2 * come[side] + half)

    def sink_start():
        x_sink(True).start()

    pl.when((x == 0) & (far != 0))(sink_start)

    lower = (left < y).astype(jnp.int32) + (right < y).astype(jnp.int32)

    @pl.when(x >= 1)
    def _():
        for half in range(2):
            x_next(2 * y + half).wait_recv()

    def own_tasks(t):
        return y, jnp.where(t < lower, 8 + jnp.where(t == 0, left, right), 4 + y)

    pipe(lower + (x >= 1).astype(jnp.int32), own_tasks)
    for half in range(2):
        for side in range(2):
            got(Q, side, half)

    def near(i):
        return i + (i >= far).astype(jnp.int32)

    loop(2, lambda t: diag(jnp.where(t == 0, left, right)))

    @pl.when(x >= 1)
    def _():
        for half in range(2):
            x_next(2 * left + half).wait_recv()

    pairs = 3 - lower
    start = ((y == 1) | (y == 2)).astype(jnp.int32)

    def near_tasks(t):
        own = t < pairs
        i = jnp.minimum(t + start, 2)
        r = t - pairs
        yq = jnp.where(
            own, near(jnp.minimum(i + 1, 2)), jnp.where(r == 0, left, jnp.where(r == 1, right, near(r - 2)))
        )
        b = jnp.where(own, 8 + near(i >> 1), 4 + jnp.where(r < 2, y, left))
        return yq, b

    pipe(pairs + jnp.where(x >= 1, 5, 0), near_tasks)

    def wrap_relays(late):
        @pl.when(relays_wrap)
        def _():
            for j in range(NM):
                i = NP + j

                @pl.when((far == i // 2) if late else (far != i // 2))
                def _():
                    x_minus(i).wait_recv()
                    x_wrap(j).start()

    wrap_relays(False)
    for half in range(2):
        got(K, 2, half)
        got(V, 2, half)
        x_send(2 * far + half)

    pl.when((x == 0) & (far == 0))(sink_start)

    @pl.when(x == 3)
    def _():
        x_sink(False).wait_recv()
        x_sink(False).start()

    @pl.when(x >= 1)
    def _():
        for half in range(2):
            x_next(2 * right + half).wait_recv()

    def right_tasks(t):
        t = t + jnp.where(x >= 1, 0, 3)
        yq = jnp.where(t < 3, near(t), near(far + t - 3))
        return yq, jnp.where(t < 3, 4 + right, 8 + far)

    pipe(jnp.where(x >= 1, 6, 3) - far, right_tasks)

    @pl.when(relays_plus)
    def _():
        @pl.when(far != 1)
        def _():
            x_plus(2).start()

        @pl.when(far >= 2)
        def _():
            x_plus(1).start()
            x_plus(0).start()

    wrap_relays(True)

    def early(b):
        return (x == 2) & (far != b)

    def wait_back(b):
        for half in range(2):
            x_wrap(2 * b + half - NP).wait_recv()

    @pl.when(two_back)
    def _():
        @pl.when(x == 2)
        def _():
            x_sink(False).wait_recv()

        loop(3, lambda t: sink_task(near(t)))

    def early_block(i):
        b = 3 - i

        @pl.when(early(b))
        def _():
            wait_back(b)
            edge(b)
            pipe(b - (far < b).astype(jnp.int32), lambda t: (near(t), b))

    loop(2, early_block)

    @pl.when(x >= 1)
    def _():
        for half in range(2):
            x_next(2 * far + half).wait_recv()

    @pl.when(relays_plus)
    def _():
        @pl.when(far == 1)
        def _():
            x_plus(2).start()

        @pl.when(far < 2)
        def _():
            x_plus(1).start()
            x_plus(0).start()

    for half in range(2):
        got(Q, 2, half)
    diag(far)

    def far_tasks(t):
        t = t + jnp.where(x >= 1, 0, 7)
        return jnp.where(t < 3, near(t), far), jnp.where(t < 3, 4 + far, t + 1)

    pipe(jnp.where(x >= 1, 7, 0) + far, far_tasks)

    pl.when(two_back)(lambda: sink_task(far))

    def late_block(i):
        b = 3 - i
        late = two_back & jnp.logical_not(early(b))

        @pl.when(late)
        def _():
            wait_back(b)
            edge(b)

        for half in range(2):
            finalize(b, half)
        for half in range(2):
            send_out(b, half)
        n = jnp.where(late, b, jnp.where(two_back & (far < b), 1, 0))
        pipe(n, lambda t: (jnp.where(late, t, far), b))

    loop(2, late_block)

    @pl.when(two_back)
    def _():
        x_wrap(3 - NP).wait_recv()
        tiles(1, 1, 3, [EDGE])

    finalize(1, 1)
    send_out(1, 1)

    @pl.when(two_back)
    def _():
        x_plus(2).wait_recv()
        tiles(1, 0, 2, [EDGE, FULL])

    finalize(1, 0)
    send_out(1, 0)

    @pl.when(two_back)
    def _():
        for half in range(2):
            tiles(0, half, 2, [FULL, FULL])
        x_plus(1).wait_recv()
        tiles(0, 1, 1, [EDGE])

    finalize(0, 1)
    send_out(0, 1)

    @pl.when(two_back)
    def _():
        tiles(0, 0, 1, [FULL])
        x_plus(0).wait_recv()
        tiles(0, 0, 0, [EDGE])

    finalize(0, 0)
    send_out(0, 0)

    for half in range(2):
        for side in range(3):
            got(O, side, half)
        own_out(half).wait()
    for p in (K, V, Q, O):
        for side in range(3):
            for half in range(2):
                send(p, side, half).wait_send()

    @pl.when(x < 3)
    def _():
        for i in range(8):
            x_next(i).wait_send()

    @pl.when(relays_plus)
    def _():
        for i in range(NP):
            x_plus(i).wait_send()

    @pl.when(x < 2)
    def _():
        for i in range(NP, 8):
            x_minus(i).wait_send()

    @pl.when(relays_wrap)
    def _():
        for j in range(NM):
            x_wrap(j).wait_send()
        x_sink(False).wait_send()


def attend(lengths, q, k, v):
    bf = jnp.bfloat16
    dma = pltpu.SemaphoreType.DMA
    any_space = pl.BlockSpec(memory_space=pl.ANY)
    return pl.pallas_call(
        kernel,
        name="window_attention",
        out_shape=jax.ShapeDtypeStruct(q.shape, bf),
        in_specs=[pl.BlockSpec(memory_space=pltpu.SMEM), any_space, any_space, any_space],
        out_specs=any_space,
        scratch_shapes=[
            pltpu.VMEM((24, 2, HALF, DIM), bf),
            pltpu.VMEM((8, 2, HALF, DIM), bf),
            pltpu.VMEM((8, 2, HALF, DIM), bf),
            pltpu.VMEM((NM, 2, HALF, DIM), bf),
            pltpu.VMEM((2, 16, DIM), bf),
            *[pltpu.VMEM((SIDE, BLOCK, DIM), jnp.float32)] * 2,
            *[pltpu.VMEM((SIDE, BLOCK, 128), jnp.float32)] * 4,
            *[pltpu.VMEM((BLOCK, BLOCK), jnp.float32)] * 2,
            dma((4, 6)), dma((4, 6)),
            dma((8,)), dma((8,)),
            dma((NP,)), dma((NP,)),
            dma((NM,)), dma((NM,)),
            dma((NM,)), dma((NM,)),
            dma((1,)), dma((1,)),
            dma((8,)),
        ],
        compiler_params=pltpu.CompilerParams(
            collective_id=0, has_side_effects=True, vmem_limit_bytes=56 * 1024 * 1024
        ),
    )(lengths, q, k, v)


def shards(queries, key_heads, projected_value_heads, lengths):
    q, k, v = (z.transpose(1, 0, 2) for z in (queries, key_heads, projected_value_heads))
    return attend(lengths, q, k, v).transpose(1, 0, 2)


def solution(mesh):
    in_specs = (
        P(("batch", "seq"), None, None),
        P(("batch", "seq"), None, None),
        P(("batch", "seq"), None, None),
        P("batch"),
    )
    out_specs = P(("batch", "seq"), None, None)
    return jax.shard_map(shards, mesh=mesh, in_specs=in_specs, out_specs=out_specs, check_vma=False)
```

time: 132 us -> 118 us (0.89); the launches traced: 131 us -> 116 us
  Pallas kernels: 121 us -> 106 us
  other arithmetic: 1.53 us -> 0 us
    pallas_call x1, Pallas kernels: 121 us -> 106 us  [attend(): pl.pallas_call(kernel, name='window_attention', out_shape=jax.ShapeDtypeS...]
    reshape x2 -> x0, local copies, waits for them, and re-layouts: 3.97 us -> none  [the longest x1 2.51 us: shards(): return out.transpose(1, 3, 0, 2, 4).reshape(tok, 2 * SIDE, DIM)]
    transpose x1 -> x2, local copies, waits for them, and re-layouts: 1.73 us -> 5.67 us  [the longest x1 4.08 us: shards(): return attend(lengths, q, k, v).transpose(1, 0, 2)]
    transpose x1 -> x0, other arithmetic: 1.53 us -> none  [shards(): kv = kv.transpose(3, 1, 0, 2, 4)]
    unnamed x7 -> x5, local copies, waits for them, and re-layouts: 2.75 us -> 3.49 us
where the time goes in v2:
time: 118 us; the launch traced here: 116 us
  Pallas kernels  106 us (90%)
  local copies, waits for them, and re-layouts  9.17 us (8%)
    pallas_call x1, Pallas kernels, attend(): pl.pallas_call(kernel, name='window_attention', out_shape=jax.ShapeDtypeS...  106 us
    transpose x1, local copies, waits for them, and re-layouts, shards(): return attend(lengths, q, k, v).transpose(1, 0, 2)  4.08 us
    unnamed x5, local copies, waits for them, and re-layouts  3.49 us

profile of v2, /device:TPU:70, one launch (start us, length us, event | category | flops | bytes accessed | tf_op | source)
XLA Modules:
  0.0 115.6 jit_solution(11483209258256025446)
XLA Ops:
  0.7 0.0 copy-start
  0.7 0.0 copy-start.1
  0.7 3.5 %copy.12 = bf16[512,8,256]{2,0,1:T(8,128)(2,1)} copy(bf16[512,8,256]{2,1,0:T(8,128)(2,1)} %param.4) | data formatting | bytes 4194304 | tf_op args[0]
  4.2 0.0 copy-done
  4.2 0.0 copy-done.1
  4.2 1.6 %copy_bitcast_fusion.1 = (bf16[4,512,256]{2,1,0:T(8,128)(2,1)}, bf16[4,512,256]{2,1,0:T(8,128)(2,1)}) fusion(bf16[512,4,256]{2,1,0:T(4,128)(2,1)S(1)} %copy-done, bf16[512,4,256]{2,1,0:T(4,128)(2,1)S(1)} %copy-done.1), kind=kLoop, calls=%fused_computation.1 | loop fusion | bytes 4194304 | tf_op jit(solution)/shard_map/transpose | solution.py:534
  5.8 105.8 %window_attention.1 = bf16[8,512,256]{2,1,0:T(8,128)(2,1)} custom-call(s32[1]{0:T(128)S(6)} %copy.13.len_ref, bf16[8,512,256]{2,1,0:T(8,128)(2,1)} %bitcast.8, bf16[4,512,256]{2,1,0:T(8,128)(2,1)} %get-tuple-element.6.k_in, bf16[4,512,256]{2,1,0:T(8,128)(2,1)} %get-tuple-element.5.v_in), custom_call_target="tpu_custom_call" | custom-call | tf_op jit(solution)/shard_map/window_attention/pallas_call | solution.py:504
  111.5 4.1 %copy.8 = bf16[512,8,256]{2,1,0:T(8,128)(2,1)} copy(bf16[512,8,256]{2,0,1:T(8,128)(2,1)} %bitcast.9) | data formatting | bytes 4194304 | tf_op jit(solution)/shard_map/transpose | solution.py:535
Async XLA Ops:
  0.7 3.5 %copy-start = (bf16[512,4,256]{2,1,0:T(4,128)(2,1)S(1)}, bf16[512,4,256]{2,1,0:T(4,128)(2,1)}, u32[]{:S(2)}) copy-start(bf16[512,4,256]{2,1,0:T(4,128)(2,1)} %param.6) | copy-start | bytes 3145732
  0.7 3.5 %copy-start.1 = (bf16[512,4,256]{2,1,0:T(4,128)(2,1)S(1)}, bf16[512,4,256]{2,1,0:T(4,128)(2,1)}, u32[]{:S(2)}) copy-start(bf16[512,4,256]{2,1,0:T(4,128)(2,1)} %param.5) | copy-start | bytes 3145732

commit v3 on v2

--- a/solution.py
+++ b/solution.py
@@ -23,7 +23,7 @@
 def kernel(
     len_ref, q_in, k_in, v_in, o_ref,
     kvb, qb, ob, rx, snk, acc0, acc1, mx0, mx1, ls0, ls1, sc0, sc1,
-    ys, yr, xs, xr, ps, pr, ms, mr, ns, nr, ss, sr, loc,
+    ys, yr, xs, xr, ps, pr, ms, mr, ns, nr, ss, sr, ks, kr, loc,
 ):
     accs, mxs, lss, scs = (acc0, acc1), (mx0, mx1), (ls0, ls1), (sc0, sc1)
     sid = lax.axis_index("seq")
@@ -89,10 +89,18 @@
     def x_wrap(j):
         return remote(rx.at[j], kvb.at[NP + j], ns.at[j], nr.at[j], dev(up, y))
 
-    def x_sink(first):
-        return remote(
-            kvb.at[16, :, pl.ds(0, 16), :] if first else snk, snk, ss.at[0], sr.at[0], dev(up, y)
-        )
+    def x_sink():
+        return remote(snk, snk, ss.at[0], sr.at[0], dev(up, y))
+
+    def sink_rows(p, n):
+        return (k_in if p == K else v_in).at[n, pl.ds(0, 16)]
+
+    def sink_out(p, side):
+        n = to[side]
+        return remote(sink_rows(p, n), snk.at[p], ks.at[p, side], kr.at[p], dev(x, n))
+
+    def sink_own(p):
+        return pltpu.make_async_copy(sink_rows(p, y), snk.at[p], loc.at[8 + p])
 
     def x_send(i):
         @pl.when(x < 3)
@@ -230,6 +238,14 @@
         for p in (K, V, Q)
         for half in range(2)
     ]
+
+    @pl.when(sid == 0)
+    def _():
+        for p in (K, V):
+            for side in range(3):
+                sink_out(p, side).start()
+            sink_own(p).start()
+
     for half in range(2):
         for side in range(2):
             send(K, side, half).start()
@@ -249,6 +265,20 @@
         mine[2 + half].wait()
         x_send(2 * y + half)
 
+    @pl.when(sid == 0)
+    def _():
+        for p in (K, V):
+            sink_own(p).wait()
+
+    @pl.when((x == 0) & (y > 0))
+    def _():
+        for p in (K, V):
+            remote(snk.at[p], snk.at[p], ks.at[p, 0], kr.at[p], dev(x, y)).wait_recv()
+
+    @pl.when(x == 0)
+    def _():
+        x_sink().start()
+
     def init(t):
         for half in range(2):
             mxs[half][t] = jnp.full((BLOCK, 128), NEG, jnp.float32)
@@ -265,10 +295,14 @@
             got(V, side, half)
             x_send(2 * come[side] + half)
 
-    def sink_start():
-        x_sink(True).start()
-
-    pl.when((x == 0) & (far != 0))(sink_start)
+    def wrap(n):
+        for half in range(2):
+            i = 2 * n + half
+
+            @pl.when(relays_wrap & (i >= NP))
+            def _():
+                x_minus(i).wait_recv()
+                x_wrap(i - NP).start()
 
     lower = (left < y).astype(jnp.int32) + (right < y).astype(jnp.int32)
 
@@ -281,6 +315,13 @@
         return y, jnp.where(t < lower, 8 + jnp.where(t == 0, left, right), 4 + y)
 
     pipe(lower + (x >= 1).astype(jnp.int32), own_tasks)
+    wrap(y)
+
+    @pl.when(x == 3)
+    def _():
+        x_sink().wait_recv()
+        x_sink().start()
+
     for half in range(2):
         for side in range(2):
             got(Q, side, half)
@@ -289,6 +330,7 @@
         return i + (i >= far).astype(jnp.int32)
 
     loop(2, lambda t: diag(jnp.where(t == 0, left, right)))
+    wrap(left)
 
     @pl.when(x >= 1)
     def _():
@@ -310,29 +352,11 @@
 
     pipe(pairs + jnp.where(x >= 1, 5, 0), near_tasks)
 
-    def wrap_relays(late):
-        @pl.when(relays_wrap)
-        def _():
-            for j in range(NM):
-                i = NP + j
-
-                @pl.when((far == i // 2) if late else (far != i // 2))
-                def _():
-                    x_minus(i).wait_recv()
-                    x_wrap(j).start()
-
-    wrap_relays(False)
+    wrap(right)
     for half in range(2):
         got(K, 2, half)
         got(V, 2, half)
         x_send(2 * far + half)
-
-    pl.when((x == 0) & (far == 0))(sink_start)
-
-    @pl.when(x == 3)
-    def _():
-        x_sink(False).wait_recv()
-        x_sink(False).start()
 
     @pl.when(x >= 1)
     def _():
@@ -357,10 +381,9 @@
             x_plus(1).start()
             x_plus(0).start()
 
-    wrap_relays(True)
 
     def early(b):
-        return (x == 2) & (far != b)
+        return (x == 2) & ((b == y) | (b == left))
 
     def wait_back(b):
         for half in range(2):
@@ -370,7 +393,7 @@
     def _():
         @pl.when(x == 2)
         def _():
-            x_sink(False).wait_recv()
+            x_sink().wait_recv()
 
         loop(3, lambda t: sink_task(near(t)))
 
@@ -401,6 +424,7 @@
             x_plus(1).start()
             x_plus(0).start()
 
+    wrap(far)
     for half in range(2):
         got(Q, 2, half)
     diag(far)
@@ -494,7 +518,13 @@
     def _():
         for j in range(NM):
             x_wrap(j).wait_send()
-        x_sink(False).wait_send()
+        x_sink().wait_send()
+
+    @pl.when(sid == 0)
+    def _():
+        for p in (K, V):
+            for side in range(3):
+                sink_out(p, side).wait_send()
 
 
 def attend(lengths, q, k, v):
@@ -522,7 +552,8 @@
             dma((NM,)), dma((NM,)),
             dma((NM,)), dma((NM,)),
             dma((1,)), dma((1,)),
-            dma((8,)),
+            dma((2, 3)), dma((2,)),
+            dma((10,)),
         ],
         compiler_params=pltpu.CompilerParams(
             collective_id=0, has_side_effects=True, vmem_limit_bytes=56 * 1024 * 1024

time: 118 us -> 109 us (0.924); the launches traced: 116 us -> 109 us
  Pallas kernels: 106 us -> 99.2 us
    pallas_call x1, Pallas kernels: 106 us -> 99.2 us  [attend(): pl.pallas_call(kernel, name='window_attention', out_shape=jax.ShapeDtypeS...]
where the time goes in v3:
time: 109 us
  Pallas kernels  99.2 us (91%)
  local copies, waits for them, and re-layouts  9.17 us (8%)
    pallas_call x1, Pallas kernels, attend(): pl.pallas_call(kernel, name='window_attention', out_shape=jax.ShapeDtypeS...  99.2 us
    transpose x1, local copies, waits for them, and re-layouts, shards(): return attend(lengths, q, k, v).transpose(1, 0, 2)  4.08 us
    unnamed x5, local copies, waits for them, and re-layouts  3.49 us

profile of v3, /device:TPU:70, one launch (start us, length us, event | category | flops | bytes accessed | tf_op | source)
XLA Modules:
  0.0 109.0 jit_solution(17927204809157370819)
XLA Ops:
  0.7 0.0 copy-start
  0.7 0.0 copy-start.1
  0.7 3.5 %copy.12 = bf16[512,8,256]{2,0,1:T(8,128)(2,1)} copy(bf16[512,8,256]{2,1,0:T(8,128)(2,1)} %param.4) | data formatting | bytes 4194304 | tf_op args[0]
  4.2 0.0 copy-done
  4.2 0.0 copy-done.1
  4.2 1.6 %copy_bitcast_fusion.1 = (bf16[4,512,256]{2,1,0:T(8,128)(2,1)}, bf16[4,512,256]{2,1,0:T(8,128)(2,1)}) fusion(bf16[512,4,256]{2,1,0:T(4,128)(2,1)S(1)} %copy-done, bf16[512,4,256]{2,1,0:T(4,128)(2,1)S(1)} %copy-done.1), kind=kLoop, calls=%fused_computation.1 | loop fusion | bytes 4194304 | tf_op jit(solution)/shard_map/transpose | solution.py:565
  5.8 99.2 %window_attention.1 = bf16[8,512,256]{2,1,0:T(8,128)(2,1)} custom-call(s32[1]{0:T(128)S(6)} %copy.13.len_ref, bf16[8,512,256]{2,1,0:T(8,128)(2,1)} %bitcast.8, bf16[4,512,256]{2,1,0:T(8,128)(2,1)} %get-tuple-element.6.k_in, bf16[4,512,256]{2,1,0:T(8,128)(2,1)} %get-tuple-element.5.v_in), custom_call_target="tpu_custom_call" | custom-call | tf_op jit(solution)/shard_map/window_attention/pallas_call | solution.py:534
  104.9 4.1 %copy.8 = bf16[512,8,256]{2,1,0:T(8,128)(2,1)} copy(bf16[512,8,256]{2,0,1:T(8,128)(2,1)} %bitcast.9) | data formatting | bytes 4194304 | tf_op jit(solution)/shard_map/transpose | solution.py:566
Async XLA Ops:
  0.7 3.5 %copy-start = (bf16[512,4,256]{2,1,0:T(4,128)(2,1)S(1)}, bf16[512,4,256]{2,1,0:T(4,128)(2,1)}, u32[]{:S(2)}) copy-start(bf16[512,4,256]{2,1,0:T(4,128)(2,1)} %param.6) | copy-start | bytes 3145732
  0.7 3.5 %copy-start.1 = (bf16[512,4,256]{2,1,0:T(4,128)(2,1)S(1)}, bf16[512,4,256]{2,1,0:T(4,128)(2,1)}, u32[]{:S(2)}) copy-start(bf16[512,4,256]{2,1,0:T(4,128)(2,1)} %param.5) | copy-start | bytes 3145732

commit v4 on v3

--- a/solution.py
+++ b/solution.py
@@ -556,7 +556,7 @@
             dma((10,)),
         ],
         compiler_params=pltpu.CompilerParams(
-            collective_id=0, has_side_effects=True, vmem_limit_bytes=56 * 1024 * 1024
+            collective_id=0, has_side_effects=True, vmem_limit_bytes=34 * 1024 * 1024
         ),
     )(lengths, q, k, v)
 

time: 109 us -> 105 us (0.963)
  local copies, waits for them, and re-layouts: 9.17 us -> 4.95 us
    transpose x1, local copies, waits for them, and re-layouts: 4.08 us -> 2.5 us  [shards(): return attend(lengths, q, k, v).transpose(1, 0, 2)]
    unnamed x5, local copies, waits for them, and re-layouts: 3.49 us -> 2.17 us
    transpose x1, local copies, waits for them, and re-layouts: 1.59 us -> 0.28 us  [shards(): z.transpose(1, 0, 2)]
where the time goes in v4:
time: 105 us
  Pallas kernels  98.9 us (94%)
  local copies, waits for them, and re-layouts  4.95 us (5%)
    pallas_call x1, Pallas kernels, attend(): pl.pallas_call(kernel, name='window_attention', out_shape=jax.ShapeDtypeS...  98.9 us
    transpose x1, local copies, waits for them, and re-layouts, shards(): return attend(lengths, q, k, v).transpose(1, 0, 2)  2.5 us
    unnamed x5, local copies, waits for them, and re-layouts  2.17 us

profile of v4, /device:TPU:70, one launch (start us, length us, event | category | flops | bytes accessed | tf_op | source)
XLA Modules:
  0.0 104.5 jit_solution(3864138402813734545)
XLA Ops:
  0.7 0.0 copy-start
  0.7 0.0 copy-start.1
  0.7 2.2 %copy.12 = bf16[512,8,256]{2,0,1:T(8,128)(2,1)S(1)} copy(bf16[512,8,256]{2,1,0:T(8,128)(2,1)} %param.4) | data formatting | bytes 4194304 | tf_op args[0]
  2.8 0.0 copy-done
  2.9 0.0 copy-done.1
  2.9 0.3 copy_bitcast_fusion.1
  3.1 98.9 %window_attention.1 = bf16[8,512,256]{2,1,0:T(8,128)(2,1)S(1)} custom-call(s32[1]{0:T(128)S(6)} %copy.13.len_ref, bf16[8,512,256]{2,1,0:T(8,128)(2,1)S(1)} %bitcast.8, bf16[4,512,256]{2,1,0:T(8,128)(2,1)S(1)} %get-tuple-element.6.k_in, bf16[4,512,256]{2,1,0:T(8,128)(2,1)S(1)} %get-tuple-element.5.v_in), custom_call_target="tpu_custom_call" | custom-call | tf_op jit(solution)/shard_map/window_attention/pallas_call | solution.py:534
  102.0 2.5 %copy.8 = bf16[512,8,256]{2,1,0:T(8,128)(2,1)} copy(bf16[512,8,256]{2,0,1:T(8,128)(2,1)S(1)} %bitcast.9) | data formatting | bytes 4194304 | tf_op jit(solution)/shard_map/transpose | solution.py:566
Async XLA Ops:
  0.7 2.2 %copy-start = (bf16[512,4,256]{2,1,0:T(4,128)(2,1)S(1)}, bf16[512,4,256]{2,1,0:T(4,128)(2,1)}, u32[]{:S(2)}) copy-start(bf16[512,4,256]{2,1,0:T(4,128)(2,1)} %param.6) | copy-start | bytes 3145732
  0.7 2.2 %copy-start.1 = (bf16[512,4,256]{2,1,0:T(4,128)(2,1)S(1)}, bf16[512,4,256]{2,1,0:T(4,128)(2,1)}, u32[]{:S(2)}) copy-start(bf16[512,4,256]{2,1,0:T(4,128)(2,1)} %param.5) | copy-start | bytes 3145732

commit v5 on v4

--- a/solution.py
+++ b/solution.py
@@ -424,7 +424,7 @@
             x_plus(1).start()
             x_plus(0).start()
 
-    wrap(far)
+    pl.when(x == 0)(lambda: wrap(far))
     for half in range(2):
         got(Q, 2, half)
     diag(far)
@@ -434,6 +434,7 @@
         return jnp.where(t < 3, near(t), far), jnp.where(t < 3, 4 + far, t + 1)
 
     pipe(jnp.where(x >= 1, 7, 0) + far, far_tasks)
+    pl.when(x == 3)(lambda: wrap(far))
 
     pl.when(two_back)(lambda: sink_task(far))
 

time: 105 us -> 102 us (0.971)
  Pallas kernels: 98.9 us -> 95.2 us
    pallas_call x1, Pallas kernels: 98.9 us -> 95.2 us  [attend(): pl.pallas_call(kernel, name='window_attention', out_shape=jax.ShapeDtypeS...]
where the time goes in v5:
time: 102 us; the launch traced here: 101 us
  Pallas kernels  95.2 us (93%)
  local copies, waits for them, and re-layouts  4.95 us (5%)
    pallas_call x1, Pallas kernels, attend(): pl.pallas_call(kernel, name='window_attention', out_shape=jax.ShapeDtypeS...  95.2 us
    transpose x1, local copies, waits for them, and re-layouts, shards(): return attend(lengths, q, k, v).transpose(1, 0, 2)  2.5 us
    unnamed x5, local copies, waits for them, and re-layouts  2.17 us

profile of v5, /device:TPU:70, one launch (start us, length us, event | category | flops | bytes accessed | tf_op | source)
XLA Modules:
  0.0 100.9 jit_solution(3892791385146930494)
XLA Ops:
  0.7 0.0 copy-start
  0.7 0.0 copy-start.1
  0.7 2.2 %copy.12 = bf16[512,8,256]{2,0,1:T(8,128)(2,1)S(1)} copy(bf16[512,8,256]{2,1,0:T(8,128)(2,1)} %param.4) | data formatting | bytes 4194304 | tf_op args[0]
  2.8 0.0 copy-done
  2.9 0.0 copy-done.1
  2.9 0.3 copy_bitcast_fusion.1
  3.1 95.2 %window_attention.1 = bf16[8,512,256]{2,1,0:T(8,128)(2,1)S(1)} custom-call(s32[1]{0:T(128)S(6)} %copy.13.len_ref, bf16[8,512,256]{2,1,0:T(8,128)(2,1)S(1)} %bitcast.8, bf16[4,512,256]{2,1,0:T(8,128)(2,1)S(1)} %get-tuple-element.6.k_in, bf16[4,512,256]{2,1,0:T(8,128)(2,1)S(1)} %get-tuple-element.5.v_in), custom_call_target="tpu_custom_call" | custom-call | tf_op jit(solution)/shard_map/window_attention/pallas_call | solution.py:535
  98.4 2.5 %copy.8 = bf16[512,8,256]{2,1,0:T(8,128)(2,1)} copy(bf16[512,8,256]{2,0,1:T(8,128)(2,1)S(1)} %bitcast.9) | data formatting | bytes 4194304 | tf_op jit(solution)/shard_map/transpose | solution.py:567
Async XLA Ops:
  0.7 2.2 %copy-start = (bf16[512,4,256]{2,1,0:T(4,128)(2,1)S(1)}, bf16[512,4,256]{2,1,0:T(4,128)(2,1)}, u32[]{:S(2)}) copy-start(bf16[512,4,256]{2,1,0:T(4,128)(2,1)} %param.6) | copy-start | bytes 3145732
  0.7 2.2 %copy-start.1 = (bf16[512,4,256]{2,1,0:T(4,128)(2,1)S(1)}, bf16[512,4,256]{2,1,0:T(4,128)(2,1)}, u32[]{:S(2)}) copy-start(bf16[512,4,256]{2,1,0:T(4,128)(2,1)} %param.5) | copy-start | bytes 3145732
